TPU v7x, 512 devices: a 8x2x16 block of a 8x8x16 slice. The times are simulated.
512 devices in a mesh: groups: 2 (over y), seq: 32 (over z, core), head: 8 (over x).
Axes of the slice: x: 8, y: 2, z: 16, core: 2. Of those that a mesh axis runs over, the one named last changes fastest.
The devices are a block of a 8x8x16 slice.
Arguments:
- queries: bfloat16 [12288, 16, 576], P(('groups', 'seq'), 'head'), parts along dimension 0, may hold values from -40 to 40
- latent_kv: bfloat16 [12288, 576], P(('groups', 'seq')), parts along dimension 0, may hold values from -6 to 6
- adapter_ids: int32 [384], P(('groups', 'seq')), parts along dimension 0, may hold values from 0 to 4
- value_up: bfloat16 [16, 512, 128], P('head'), may hold values from -0.25 to 0.25
- output_weight: bfloat16 [2048, 2048], P('head'), may hold values from -0.1875 to 0.1875
- adapter_down: bfloat16 [2048, 80], P('head'), may hold values from -0.125 to 0.125
- adapter_up: bfloat16 [80, 2048], replicated, may hold values from -1.5 to 1.5
Outputs:
- mixed: bfloat16 [12288, 2048], P(('groups', 'seq'), 'head'), parts along dimension 0
There are 2 independent parts, one for each index of `groups`. A program takes and returns all parts, laid end to end along the dimension named above; an argument that names none is the same for every part. Nothing has to cross between parts.
All inputs are finite; a program needn't handle non-finite values.
Results may differ from a plain program's by a relative error of at most 0.017.
Values may be sent and summed in bfloat16 or wider, within the bound.
A program may use at most 64 MiB of HBM per device.

v0:
```python
import math

import jax
import jax.numpy as jnp
from jax import lax
from jax.sharding import PartitionSpec as P

ROPE = 64
NOPE = 128
ADAPTERS = 5
RANK = 16
ADP_BLOCK = 32


def split_up(array, dim, peers):
    shape = array.shape
    parts = array.reshape(*shape[:dim], peers, shape[dim] // peers, *shape[dim + 1 :])
    return jnp.moveaxis(parts, dim, 0)


def summed_on_arrival(array, axis, dim):
    peers = lax.axis_size(axis)
    parts = lax.all_to_all(split_up(array, dim, peers), axis, 0, 0, tiled=True)
    return jnp.sum(parts.astype(jnp.float32), axis=0)


def mirror_position(rows, tok_dev, count):
    shard = rows // tok_dev
    within = rows % tok_dev
    half = tok_dev // 2
    return jnp.where(
        within < half, shard * half + within, (2 * count - 1 - shard) * half + within - half
    )


def attend(totals, query_rows, row_position, carried, key_position, score_scale, latent_dim):
    row_max, row_sum, accumulated = totals
    scores = (
        lax.dot_general(
            query_rows, carried, (((1,), (1,)), ((), ())), preferred_element_type=jnp.float32
        )
        * score_scale
    )
    visible = key_position[None, :] <= row_position[:, None]
    scores = jnp.where(visible, scores, -1e30)
    new_max = jnp.maximum(row_max, jnp.max(scores, axis=1))
    weights = jnp.exp(scores - new_max[:, None])
    row_sum = jnp.sum(weights, axis=1)
    product = jnp.dot(
        weights.astype(jnp.bfloat16), carried[:, :latent_dim], preferred_element_type=jnp.float32
    )
    accumulated = product
    return (new_max, row_sum, accumulated)


def body(queries, latent_kv, adapter_ids, value_up, output_weight, adapter_down, adapter_up):
    seq_count = lax.axis_size("seq")
    own_index = lax.axis_index("seq")
    tok_rows = queries.shape[0]
    head_count = queries.shape[1]
    latent_width = latent_kv.shape[1]
    latent_dim = value_up.shape[1]
    score_scale = 1.0 / math.sqrt(NOPE + ROPE)
    query_rows = queries.reshape(tok_rows * head_count, latent_width)
    row_position = mirror_position(
        own_index * tok_rows + jnp.arange(tok_rows * head_count, dtype=jnp.int32) // head_count,
        tok_rows,
        seq_count,
    )
    start = (
        jnp.full((tok_rows * head_count,), -1e30, jnp.float32),
        jnp.zeros((tok_rows * head_count,), jnp.float32),
        jnp.zeros((tok_rows * head_count, latent_dim), jnp.float32),
    )
    carried = lax.all_gather(latent_kv, "seq", axis=0, tiled=True)
    key_position = mirror_position(
        jnp.arange(carried.shape[0], dtype=jnp.int32), tok_rows, seq_count
    )
    key_position = jnp.where(True, key_position, 2**30)
    totals = attend(start, query_rows, row_position, carried, key_position, score_scale, latent_dim)
    latent_out = (
        (totals[2] / totals[1][:, None])
        .astype(jnp.bfloat16)
        .reshape(tok_rows, head_count, latent_dim)
    )
    value_out = jnp.einsum("thl,hlv->thv", latent_out, value_up, preferred_element_type=jnp.float32)
    value_out = value_out.astype(jnp.bfloat16).reshape(tok_rows, head_count * value_up.shape[2])
    projected = jnp.dot(value_out, output_weight, preferred_element_type=jnp.float32)
    rank_part = jnp.dot(value_out, adapter_down, preferred_element_type=jnp.float32)
    owner = jnp.arange(ADAPTERS * RANK, dtype=jnp.int32) // RANK
    block_count = adapter_ids.shape[0]
    selector = (adapter_ids[:, None, None] == owner[None, None, :]).astype(jnp.float32)
    selector = jnp.broadcast_to(selector, (block_count, ADP_BLOCK, ADAPTERS * RANK)).reshape(
        tok_rows, ADAPTERS * RANK
    )
    partial_value = projected + jnp.dot(
        rank_part * selector, adapter_up.astype(jnp.float32), precision=lax.Precision.HIGHEST
    )
    mixed = summed_on_arrival(partial_value.astype(jnp.bfloat16), "head", 1)
    return mixed.astype(jnp.bfloat16)


def solution(mesh):
    return jax.shard_map(
        body,
        mesh=mesh,
        in_specs=(
            P(("groups", "seq"), "head", None),
            P(("groups", "seq"), None),
            P(("groups", "seq")),
            P("head", None, None),
            P("head", None),
            P("head", None),
            P(),
        ),
        out_specs=P(("groups", "seq"), "head"),
        check_vma=False,
    )
```

profile of v0, /device:TPU:80, one launch (start us, length us, event | category | flops | bytes accessed | tf_op | source)
XLA Modules:
  0.0 174.9 jit_solution(4490372963135082151)
XLA Ops:
  6.5 0.0 copy-start
  6.6 0.0 all-gather.2.cloned.1.call-start
  6.6 0.7 all-gather.2.cloned.1.call-update
  7.3 1.4 reshape.122
  8.7 0.7 compare_convert_fusion
  9.5 0.1 copy.16
  9.6 113.0 %all-gather.2.cloned.1.call-done = bf16[6144,576]{1,0:T(8,128)(2,1)} async-done(((bf16[192,576]{1,0:T(8,128)(2,1)}), bf16[6144,576]{1,0:T(8,128)(2,1)}) %all-gather.2.cloned.1.call-update) | async-done | bytes 7077904 | tf_op jit(solution)/shard_map/all_gather | solution.py:75
  122.6 6.7 %fusion.41 = (f32[384]{0:T(512)S(1)}, f32[384,6144]{1,0:T(8,128)S(1)}) fusion(bf16[384,576]{1,0:T(8,128)(2,1)S(1)} %reshape.122, bf16[6144,576]{1,0:T(8,128)(2,1)} %all-gather.2.cloned.1.call-done, s32[384]{0:T(512)S(1)} %add_select_fusion.4, s32[6144]{0:T(1024)S(1)} %fusion.33), kind=kOutput, calls=%fused_computation.57 | convolution fusion | flops 2727345664 | bytes 16985088 | tf_op jit(solution)/shard_map/dot_general | solution.py:39
  129.3 0.0 copy-start.3
  129.3 1.4 fusion
  130.8 1.8 %copy-done.3 = bf16[6144,576]{1,0:T(8,128)(2,1)S(1)} copy-done((bf16[6144,576]{1,0:T(8,128)(2,1)S(1)}, bf16[6144,576]{1,0:T(8,128)(2,1)}, u32[]{:S(2)}) %copy-start.3) | copy-done | bytes 7077912
  132.5 0.0 copy-start.4
  132.5 0.0 copy-start.2
  132.5 0.0 copy-start.1
  132.5 2.8 %fusion.12 = bf16[384,512]{1,0:T(8,128)(2,1)S(1)} fusion(bf16[6144,576]{1,0:T(8,128)(2,1)S(1)} %copy-done.3, f32[384,6144]{1,0:T(8,128)S(1)} %get-tuple-element.6, f32[384]{0:T(512)S(1)} %broadcast_maximum_fusion, f32[384]{0:T(512)S(1)} %fusion), kind=kOutput, calls=%fused_computation.10 | convolution fusion | flops 2421030912 | bytes 16125952 | tf_op jit(solution)/shard_map/dot_general | solution.py:49
  135.3 0.2 reshape.123
  135.5 0.0 copy-done.4
  135.5 0.3 fusion.17
  135.8 0.0 copy-done
  135.8 0.4 fusion.20
  136.2 0.0 copy-done.2
  136.2 0.2 convolution_multiply_fusion
  136.3 0.0 copy-done.1
  136.4 0.8 fusion.6
  137.2 0.1 copy.31
  137.3 30.0 %all_to_all.5 = bf16[8,192,256]{2,1,0:T(8,128)(2,1)S(1)} all-to-all(bf16[8,192,256]{2,1,0:T(8,128)(2,1)S(1)} %bitcast.23), channel_id=1, replica_groups=mesh['groups'=2,'seq'=32,'head'=8] {'head'}, dimensions={0} | all-to-all | bytes 1572864 | tf_op jit(solution)/shard_map/all_to_all | solution.py:23
  167.3 0.8 reduce_sum.22
  (5 shorter events, 0.1 us)
Async XLA Ops:
  6.5 129.2 %copy-start = (bf16[256,2048]{1,0:T(8,128)(2,1)S(1)}, bf16[256,2048]{1,0:T(8,128)(2,1)}, u32[]{:S(2)}) copy-start(bf16[256,2048]{1,0:T(8,128)(2,1)} %param.11) | copy-start | bytes 3145732
  6.6 116.0 %all-gather.2.cloned.1.call-start = ((), (), s32[]{:S(2)}) async-start(), calls=%async_computation.1 | async-start | bytes 8110080 | tf_op jit(solution)/shard_map/all_gather | solution.py:75
  129.3 3.2 %copy-start.3 = (bf16[6144,576]{1,0:T(8,128)(2,1)S(1)}, bf16[6144,576]{1,0:T(8,128)(2,1)}, u32[]{:S(2)}) copy-start(bf16[6144,576]{1,0:T(8,128)(2,1)} %all-gather.2.cloned.1.call-done) | copy-start | bytes 21233668
  132.5 3.0 %copy-start.4 = (bf16[2,512,128]{2,1,0:T(8,128)(2,1)S(1)}, bf16[2,512,128]{2,1,0:T(8,128)(2,1)}, u32[]{:S(2)}) copy-start(bf16[2,512,128]{2,1,0:T(8,128)(2,1)} %param.10) | copy-start | bytes 786436
  132.5 3.6 %copy-start.2 = (bf16[256,80]{0,1:T(8,128)(2,1)S(1)}, bf16[256,80]{0,1:T(8,128)(2,1)}, u32[]{:S(2)}) copy-start(bf16[256,80]{0,1:T(8,128)(2,1)} %param.12) | copy-start | bytes 122884
  132.5 3.8 %copy-start.1 = (bf16[80,2048]{1,0:T(8,128)(2,1)S(1)}, bf16[80,2048]{1,0:T(8,128)(2,1)}, u32[]{:S(2)}) copy-start(bf16[80,2048]{1,0:T(8,128)(2,1)} %param.13) | copy-start | bytes 983044
Sparse Core Ops, SparseCore 0:
  9.5 113.0 all-gather.1
where the time goes:
time: 177 us; the launch traced here: 175 us
  waiting for transfers between devices  114 us (64%)
  blocking collectives  30 us (17%)
  between operations  13.6 us (8%)
  matrix products  11.1 us (6%)
  local copies, waits for them, and re-layouts  3.5 us (2%)
  other arithmetic  2.97 us (2%)
    all_gather x1, waiting for transfers between devices, body(): carried = lax.all_gather(latent_kv, 'seq', axis=0, tiled=True)  113 us
    all_to_all x1, blocking collectives, summed_on_arrival(): parts = lax.all_to_all(split_up(array, dim, peers), axis, 0, 0, tiled=True)  30 us
    dot_general x1, matrix products, attend(): lax.dot_general(query_rows, carried, (((1,), (1,)), ((), ())), preferred_...  6.7 us
  transfers between devices with their start and end apart: 1, of which 1 were waited for; matrix products, arithmetic and copies ran while one was open for 1% of the time, Pallas kernels for 0%

commit v1 on v0

v1 whole, which is shorter than its diff:
```python
import functools
import math

import jax
import jax.numpy as jnp
from jax import lax
from jax.experimental import pallas as pl
from jax.experimental.pallas import tpu as pltpu
from jax.sharding import PartitionSpec as P

ROPE = 64
NOPE = 128
ADAPTERS = 5
RANK = 16
ADP_BLOCK = 32
UNIT = 16
BF16 = jnp.bfloat16
F32 = jnp.float32
MESH = pl.DeviceIdType.MESH


def kernel(
    cfg,
    ids_ref,
    q_hbm,
    kv_ref,
    vup_hbm,
    w_hbm,
    down_hbm,
    up_hbm,
    out_ref,
    buf,
    q_ref,
    vup_ref,
    w_ref,
    down_ref,
    up_ref,
    m_ref,
    l_ref,
    acc_ref,
    part_ref,
    sum_ref,
    rs_ref,
    load_sem,
    send_sem,
    z_sem,
    x_sem,
    c_sem,
    rs_send,
    rs_sem,
):
    rows_z, n_x, half, latent, vhead = cfg
    pack = half // 2
    units = pack // UNIT
    reach = rows_z // 2
    wide = 2 * latent
    scale = math.log2(math.e) / math.sqrt(NOPE + ROPE)
    heads = q_ref.shape[1] // half
    nodes = 2 * rows_z

    seq = lax.axis_index("seq")
    x = lax.axis_index("head")
    z, core = seq // 2, seq % 2
    sigma = 1 - 2 * core
    parity = x % 2

    def row(delta):
        return (z + delta + 2 * rows_z) % rows_z

    def col(delta):
        return (x + delta + 2 * n_x) % n_x

    def chunk(zz, cc, late):
        s = 2 * zz + cc
        return s + late * (2 * nodes - 1 - 2 * s)

    ahead = {"seq": 2 * row(sigma) + core}
    behind = {"seq": 2 * row(-sigma) + core}
    sibling = {"seq": 2 * z + 1 - core}
    x_ahead = {"head": col(sigma)}
    x_behind = {"head": col(-sigma)}

    loads = [
        pltpu.make_async_copy(src, dst, load_sem.at[i])
        for i, (src, dst) in enumerate(
            (
                (q_hbm, q_ref),
                (vup_hbm, vup_ref),
                (w_hbm, w_ref),
                (down_hbm, down_ref),
                (up_hbm, up_ref),
            )
        )
    ]
    for load in loads:
        load.start()

    for late in (0, 1):
        own = kv_ref[late * half : (late + 1) * half, :]
        first, second = own[:pack], own[pack:]
        c = chunk(z, core, late)
        buf[c, :, :latent] = first[:, :latent]
        buf[c, :, latent:wide] = second[:, :latent]
        buf[c, :, wide:] = jnp.concatenate([first[:, latent:], second[:, latent:]], axis=1)

    barrier = pltpu.get_barrier_semaphore()
    pl.semaphore_signal(barrier, inc=1, device_id=sibling, device_id_type=MESH)
    for peer in (ahead, behind, x_ahead, x_behind):
        pl.semaphore_signal(barrier, inc=1, device_id=peer, device_id_type=MESH)
    pl.semaphore_wait(barrier, 5)

    def push(ref, send, recv, peer):
        pltpu.make_async_remote_copy(
            src_ref=ref, dst_ref=ref, send_sem=send, recv_sem=recv, device_id=peer, device_id_type=MESH
        ).start()

    def arrived(ref, recv):
        pltpu.make_async_copy(ref, ref, recv).wait()

    def unit(c, j):
        return buf.at[c, pl.ds(j * UNIT, UNIT)]

    AHEAD, BEHIND, XA, XB, SIB = range(5)

    own = chunk(z, core, parity)
    for j in range(units):
        push(unit(own, j), send_sem.at[AHEAD], z_sem.at[z, j], ahead)
        push(unit(own, j), send_sem.at[BEHIND], z_sem.at[z, j], behind)
    for late in (0, 1):
        push(buf.at[chunk(z, core, late)], send_sem.at[SIB], c_sem.at[z, late], sibling)

    def from_z(zz, j, onward, slot):
        c = chunk(zz, core, parity)
        piece = unit(c, j)
        arrived(piece, z_sem.at[zz, j])
        if onward is not None:
            push(piece, send_sem.at[slot], z_sem.at[zz, j], onward)
        if j == 0:
            push(piece, send_sem.at[XB], x_sem.at[zz, j], x_behind)
        else:
            push(piece, send_sem.at[XA], x_sem.at[zz, j], x_ahead)
        push(piece, send_sem.at[SIB], c_sem.at[zz, parity], sibling)

    def from_x(zz, j):
        piece = unit(chunk(zz, core, 1 - parity), j)
        arrived(piece, x_sem.at[zz, j])
        push(piece, send_sem.at[SIB], c_sem.at[zz, 1 - parity], sibling)

    def from_sibling(zz):
        for late in (0, 1):
            arrived(buf.at[chunk(zz, 1 - core, late)], c_sem.at[zz, late])

    def keys(base):
        pair = buf[pl.ds(base, 2)].reshape(2 * pack, wide + 2 * ROPE)
        value = jnp.concatenate([pair[:, :latent], pair[:, latent:wide]], axis=0)
        turned = jnp.concatenate([pair[:, wide : wide + ROPE], pair[:, wide + ROPE :]], axis=0)
        return value, turned

    def attend(which, bases, mask_shift=None, first=False):
        got = [keys(b) for b in bases]
        value = jnp.concatenate([g[0] for g in got], axis=0) if len(got) > 1 else got[0][0]
        turned = jnp.concatenate([g[1] for g in got], axis=0) if len(got) > 1 else got[0][1]
        nt = (((1,), (1,)), ((), ()))
        s = lax.dot_general(
            q_ref[which, :, :latent], value, nt, preferred_element_type=F32
        ) + lax.dot_general(q_ref[which, :, latent:], turned, nt, preferred_element_type=F32)
        if mask_shift is not None:
            n = lax.broadcasted_iota(jnp.int32, s.shape, 1)
            i = lax.broadcasted_iota(jnp.int32, s.shape, 0) % half
            at = ((n % (2 * pack)) // pack) * half + (n // (2 * pack)) * pack + n % pack
            s = jnp.where(at <= i + mask_shift, s, -1e30)
        top = jnp.max(s, axis=1, keepdims=True)
        if first:
            m = top
        else:
            old = m_ref[which][:, :1]
            m = jnp.maximum(old, top)
            decay = jnp.exp2((old - m) * scale)
        w = jnp.exp2((s - m) * scale)
        total = jnp.sum(w, axis=1, keepdims=True)
        new = jnp.dot(w.astype(BF16), value, preferred_element_type=F32)
        if not first:
            total = total + l_ref[which][:, :1] * decay
            new = new + acc_ref[which] * decay
        m_ref[which] = jnp.broadcast_to(m, m_ref.shape[1:])
        l_ref[which] = jnp.broadcast_to(total, l_ref.shape[1:])
        acc_ref[which] = new

    def low(zz):
        return 2 * zz

    def high(zz):
        return 2 * nodes - 2 - 2 * zz

    def extra(t, sign):
        raw = z + sign * t
        zz = (raw + rows_z) % rows_z
        before = jnp.where(zz < z, 1, 0)
        attend(1 - before, [low(zz) + (1 - before) * (high(zz) - low(zz))])

    def compute(t):
        from_sibling(row(-t))
        from_sibling(row(t))
        attend(1, [low(row(-t)), low(row(t))])
        extra(t, -1)
        extra(t, 1)

    def step_z(t, last_behind=False):
        for j in range(units):
            from_z(row(-sigma * t), j, ahead, AHEAD)
            from_z(row(sigma * t), j, None if last_behind else behind, BEHIND)

    def step_x(t):
        for j in range(units):
            from_x(row(-sigma * t), j)
            from_x(row(sigma * t), j)

    loads[0].wait()
    from_sibling(z)
    attend(1, [high(z)], mask_shift=(1 - core) * half, first=True)
    attend(0, [low(z)], mask_shift=core * half, first=True)
    attend(1, [low(z)])

    step_z(1)
    step_z(2)
    step_x(1)

    def body(t, carry):
        step_z(t)
        step_x(t - 1)
        compute(t - 2)
        return carry

    lax.fori_loop(3, reach - 1, body, 0)
    step_z(reach - 1, last_behind=True)
    step_x(reach - 2)
    compute(reach - 3)
    far = row(reach)
    for j in range(units):
        from_z(far, j, None, None)
    step_x(reach - 1)
    compute(reach - 2)
    for j in range(units):
        from_x(far, j)
    compute(reach - 1)
    from_sibling(far)
    attend(1, [low(far)])
    before = jnp.where(far < z, 1, 0)
    attend(1 - before, [low(far) + (1 - before) * (high(far) - low(far))])

    for load in loads[1:]:
        load.wait()

    features = w_ref.shape[1]
    share = features // n_x

    def project(which):
        o = acc_ref[which] * (1.0 / l_ref[which][:, :1])
        o = o.astype(BF16)
        vo = jnp.concatenate(
            [
                jnp.dot(o[h * half : (h + 1) * half], vup_ref[h], preferred_element_type=F32).astype(BF16)
                for h in range(heads)
            ],
            axis=1,
        )
        rank = jnp.dot(vo, down_ref[...], preferred_element_type=F32)
        r = lax.broadcasted_iota(jnp.int32, rank.shape, 0) // ADP_BLOCK
        owner = lax.broadcasted_iota(jnp.int32, rank.shape, 1) // RANK
        blocks = half // ADP_BLOCK
        pick = jnp.zeros(rank.shape, jnp.int32)
        for b in range(blocks):
            pick = jnp.where(r == b, ids_ref[which * blocks + b], pick)
        chosen = jnp.where(owner == pick, rank, 0.0)
        hi = chosen.astype(BF16)
        rest = chosen - hi.astype(F32)
        mid = rest.astype(BF16)
        lo = (rest - mid.astype(F32)).astype(BF16)
        for d in range(n_x):
            cols = slice(d * share, (d + 1) * share)
            up = up_ref[:, cols]
            y = jnp.dot(vo, w_ref[:, cols], preferred_element_type=F32)
            y = y + (
                jnp.dot(hi, up, preferred_element_type=F32)
                + jnp.dot(mid, up, preferred_element_type=F32)
                + jnp.dot(lo, up, preferred_element_type=F32)
            )
            part_ref[which, d] = y.astype(BF16)

    far_x = n_x // 2

    def rs_push(ref, which, way, k):
        pltpu.make_async_remote_copy(
            src_ref=ref,
            dst_ref=rs_ref.at[which, way, k],
            send_sem=rs_send.at[way],
            recv_sem=rs_sem.at[which, way, k],
            device_id=x_ahead if way == 0 else x_behind,
            device_id_type=MESH,
        ).start()

    for which in (0, 1):
        project(which)
        rs_push(part_ref.at[which, col(sigma * far_x)], which, 0, 0)
        rs_push(part_ref.at[which, col(-sigma * (far_x - 1))], which, 1, 0)

    for k in range(1, far_x):
        for which in (0, 1):
            for way in (0, 1):
                hops = far_x - way - k
                if hops < 1:
                    continue
                arrived(rs_ref.at[which, way, k - 1], rs_sem.at[which, way, k - 1])
                dest = col((sigma if way == 0 else -sigma) * hops)
                sum_ref[which, way, k] = (
                    rs_ref[which, way, k - 1].astype(F32) + part_ref[which, dest].astype(F32)
                ).astype(BF16)
                rs_push(sum_ref.at[which, way, k], which, way, k)

    for which in (0, 1):
        for way in (0, 1):
            k = far_x - 1 - way
            arrived(rs_ref.at[which, way, k], rs_sem.at[which, way, k])
        out_ref[which * half : (which + 1) * half, :] = (
            part_ref[which, x].astype(F32)
            + rs_ref[which, 0, far_x - 1].astype(F32)
            + rs_ref[which, 1, far_x - 2].astype(F32)
        ).astype(BF16)

    def drained(ref, sem):
        pltpu.make_async_copy(ref, ref, sem).wait()

    others = rows_z - 1
    drained(buf.at[pl.ds(0, reach)], send_sem.at[AHEAD])
    drained(buf.at[pl.ds(0, reach - 1)], send_sem.at[BEHIND])
    drained(buf.at[pl.ds(0, others), pl.ds(0, UNIT)], send_sem.at[XB])
    drained(buf.at[pl.ds(0, others), pl.ds(0, pack - UNIT)], send_sem.at[XA])
    drained(buf.at[pl.ds(0, 2 * rows_z)], send_sem.at[SIB])
    for way in (0, 1):
        drained(rs_ref.at[:, way, pl.ds(0, far_x - way)], rs_send.at[way])


def body(n_seq, n_x, queries, latent_kv, adapter_ids, value_up, output_weight, adapter_down, adapter_up):
    tok, heads, width = queries.shape
    latent, vhead = value_up.shape[1:]
    half = tok // 2
    q = queries.reshape(2, half, heads, width).swapaxes(1, 2).reshape(2, heads * half, width)
    features = output_weight.shape[1]
    share = features // n_x
    rows_z = n_seq // 2
    far_x = n_x // 2
    pack = half // 2
    any_spec = pl.BlockSpec(memory_space=pl.ANY)
    vmem = pl.BlockSpec(memory_space=pltpu.VMEM)
    return pl.pallas_call(
        functools.partial(kernel, (rows_z, n_x, half, latent, vhead)),
        out_shape=jax.ShapeDtypeStruct((tok, share), BF16),
        in_specs=[pl.BlockSpec(memory_space=pltpu.SMEM), any_spec, vmem, any_spec, any_spec, any_spec, any_spec],
        out_specs=vmem,
        scratch_shapes=[
            pltpu.VMEM((2 * n_seq, pack, 2 * width), BF16),
            pltpu.VMEM(q.shape, BF16),
            pltpu.VMEM(value_up.shape, BF16),
            pltpu.VMEM(output_weight.shape, BF16),
            pltpu.VMEM(adapter_down.shape, BF16),
            pltpu.VMEM(adapter_up.shape, BF16),
            pltpu.VMEM((2, heads * half, 128), F32),
            pltpu.VMEM((2, heads * half, 128), F32),
            pltpu.VMEM((2, heads * half, latent), F32),
            pltpu.VMEM((2, n_x, half, share), BF16),
            pltpu.VMEM((2, 2, far_x, half, share), BF16),
            pltpu.VMEM((2, 2, far_x, half, share), BF16),
            pltpu.SemaphoreType.DMA((5,)),
            pltpu.SemaphoreType.DMA((5,)),
            pltpu.SemaphoreType.DMA((rows_z, pack // UNIT)),
            pltpu.SemaphoreType.DMA((rows_z, pack // UNIT)),
            pltpu.SemaphoreType.DMA((rows_z, 2)),
            pltpu.SemaphoreType.DMA((2,)),
            pltpu.SemaphoreType.DMA((2, 2, far_x)),
        ],
        compiler_params=pltpu.CompilerParams(
            collective_id=0, has_side_effects=True, vmem_limit_bytes=56 * 1024 * 1024
        ),
    )(adapter_ids, q, latent_kv, value_up, output_weight, adapter_down, adapter_up)


def solution(mesh):
    return jax.shard_map(
        functools.partial(body, mesh.shape["seq"], mesh.shape["head"]),
        mesh=mesh,
        in_specs=(
            P(("groups", "seq"), "head", None),
            P(("groups", "seq"), None),
            P(("groups", "seq")),
            P("head", None, None),
            P("head", None),
            P("head", None),
            P(),
        ),
        out_specs=P(("groups", "seq"), "head"),
        check_vma=False,
    )
```

time: 177 us -> 106 us (0.60)
  waiting for transfers between devices: 114 us -> 0 us
  Pallas kernels: 0 us -> 100 us
  blocking collectives: 30 us -> 0 us
  between operations: 13.6 us -> 0.01 us
  matrix products: 11.1 us -> 0 us
  other arithmetic: 2.97 us -> 0 us
    all_gather x1 -> x0, waiting for transfers between devices: 113 us -> none  [body(): carried = lax.all_gather(latent_kv, 'seq', axis=0, tiled=True)]
    pallas_call x0 -> x1, Pallas kernels: none -> 100 us  [body(): pl.pallas_call(functools.partial(kernel, (rows_z, n_x, half, latent, vhea...]
    all_to_all x1 -> x0, blocking collectives: 30 us -> none  [summed_on_arrival(): parts = lax.all_to_all(split_up(array, dim, peers), axis, 0, 0, tiled=True)]
    dot_general x6 -> x0, matrix products: 11.1 us -> none  [the longest x1 6.7 us: attend(): lax.dot_general(query_rows, carried, (((1,), (1,)), ((), ())), preferred_...]
    reduce_sum x2 -> x0, other arithmetic: 2.19 us -> none  [the longest x1 1.44 us: attend(): row_sum = jnp.sum(weights, axis=1)]
  transfers between devices with their start and end apart: 1 -> 0, of which waited for: 1 -> 0; matrix products, arithmetic and copies ran while one was open for 1% -> 0% of each run, Pallas kernels for 0% -> 0%
where the time goes in v1:
time: 106 us; the launch traced here: 105 us
  Pallas kernels  100 us (94%)
  local copies, waits for them, and re-layouts  4.9 us (5%)
    pallas_call x1, Pallas kernels, body(): pl.pallas_call(functools.partial(kernel, (rows_z, n_x, half, latent, vhea...  100 us
    unnamed x2, local copies, waits for them, and re-layouts  3.05 us

profile of v1, /device:TPU:80, one launch (start us, length us, event | category | flops | bytes accessed | tf_op | source)
XLA Modules:
  0.0 105.2 jit_solution(6998644660052579049)
XLA Ops:
  0.0 1.5 %copy.9.down_hbm = bf16[256,80]{1,0:T(8,128)(2,1)} copy(bf16[256,80]{0,1:T(8,128)(2,1)} %param.12) | data formatting | bytes 81920 | tf_op args[5]
  1.5 1.9 %copy.8 = bf16[2,96,2,576]{3,1,2,0:T(8,128)(2,1)} copy(bf16[2,96,2,576]{3,2,1,0:T(2,128)(2,1)} %bitcast.5) | data formatting | bytes 884736 | tf_op jit(solution)/shard_map/reshape | solution.py:347
  3.4 100.3 %shard_map.73 = bf16[192,256]{1,0:T(8,128)(2,1)} custom-call(s32[6]{0:T(128)} %ids_ref.1, bf16[2,192,576]{2,1,0:T(8,128)(2,1)} %bitcast.4, bf16[192,576]{1,0:T(8,128)(2,1)} %kv_ref.1, bf16[2,512,128]{2,1,0:T(8,128)(2,1)} %vup_hbm.1, bf16[256,2048]{1,0:T(8,128)(2,1)} %w_hbm.1, bf16[256,80]{1,0:T(8,128)(2,1)} %copy.9.down_hbm, bf16[80,2048]{1,0:T(8,128)(2,1)} %up_hbm.1), custom_call_target="tpu_custom_call" | custom-call | tf_op jit(solution)/shard_map/pallas_call | solution.py:355
  103.6 1.5 %copy.11 = bf16[192,256]{1,0:T(8,128)(2,1)} copy(bf16[192,256]{1,0:T(8,128)(2,1)} %shard_map.73) | data formatting | bytes 196608
